TPU v7x, 8 devices: a whole 2x2x1 slice. The times are simulated.
8 devices in a mesh: dp: 2 (over z, y), fsdp: 4 (over x, core).
Axes of the slice: x: 2, y: 2, z: 1, core: 2. Of those that a mesh axis runs over, the one named last changes fastest.
Arguments:
- hidden: bfloat16 [8192, 512], P(('dp', 'fsdp')), parts along dimension 0
- targets: int32 [8192], P(('dp', 'fsdp')), parts along dimension 0
- weight: bfloat16 [32128, 512], P('fsdp')
Outputs:
- output 1: float32 [2], P('dp'), parts along dimension 0
- output 2: float32 [8192, 512], P(('dp', 'fsdp')), parts along dimension 0
- output 3: float32 [64256, 512], P(('dp', 'fsdp')), parts along dimension 0
There are 2 independent parts. A program takes and returns all parts, laid end to end along the dimension named above; an argument that names none is the same for every part.
All inputs are finite; a program needn't handle non-finite values.
Results may differ from a plain program's by a relative error of at most 0.001.
Values are sent between devices in bfloat16 or wider.
A program may use at most 1 GiB of HBM per device.

v0:
```python
import jax
import jax.numpy as jnp
from jax import lax
from jax.sharding import PartitionSpec as P


def solution(mesh):
    groups = mesh.shape["fsdp"]
    ring_pairs = [(src_idx, (src_idx + 1) % groups) for src_idx in range(groups)]
    tok_spec = P(("dp", "fsdp"), None)

    def local_head(hidden, targets, weight):
        tok_loc = hidden.shape[0]
        shard_rows = weight.shape[0]
        tokens = tok_loc * groups
        rank_id = lax.axis_index("fsdp")
        col_ids = jnp.arange(shard_rows, dtype=jnp.int32)

        def block_logits(w_blk, step_idx):
            owner_idx = (rank_id - step_idx) % groups
            logits = lax.dot_general(hidden, w_blk, (((1,), (1,)), ((), ())), preferred_element_type=jnp.float32)
            is_target = (targets - owner_idx * shard_rows)[:, None] == col_ids[None, :]
            return logits, is_target

        def fwd_update(fwd_state, w_blk, step_idx):
            run_max, run_sum, tgt_logit = fwd_state
            logits, is_target = block_logits(w_blk, step_idx)
            new_max = jnp.maximum(run_max, jnp.max(logits, axis=1))
            run_sum = run_sum * jnp.exp(run_max - new_max) + jnp.sum(jnp.exp(logits - new_max[:, None]), axis=1)
            tgt_logit = tgt_logit + jnp.sum(jnp.where(is_target, logits, 0.0), axis=1)
            return new_max, run_sum, tgt_logit

        def fwd_body(step_idx, loop_state):
            w_cur, fwd_state = loop_state
            w_cur = lax.ppermute(w_cur, "fsdp", ring_pairs)
            return w_cur, fwd_update(fwd_state, w_cur, step_idx)

        init_state = (jnp.full((tok_loc,), -jnp.inf, jnp.float32), jnp.zeros((tok_loc,), jnp.float32), jnp.zeros((tok_loc,), jnp.float32))
        first_state = fwd_update(init_state, weight, 0)
        run_max, run_sum, tgt_logit = lax.fori_loop(1, groups, fwd_body, (weight, first_state))[1]
        log_norm = run_max + jnp.log(run_sum)
        loss_val = lax.psum(jnp.sum(log_norm - tgt_logit) / tokens, "fsdp").reshape(1)

        def bwd_update(w_blk, step_idx):
            logits, is_target = block_logits(w_blk, step_idx)
            dlogits = ((jnp.exp(logits - log_norm[:, None]) - is_target.astype(jnp.float32)) / tokens).astype(jnp.bfloat16)
            dh_part = jnp.dot(dlogits, w_blk, preferred_element_type=jnp.float32)
            dw_part = lax.dot_general(dlogits, hidden, (((0,), (0,)), ((), ())), preferred_element_type=jnp.float32)
            return dh_part, dw_part

        def bwd_body(step_idx, loop_state):
            w_cur, dw_acc, grad_h = loop_state
            w_cur = lax.ppermute(w_cur, "fsdp", ring_pairs)
            dw_acc = lax.ppermute(dw_acc, "fsdp", ring_pairs)
            dh_part, dw_part = bwd_update(w_cur, step_idx)
            return w_cur, dw_acc + dw_part, grad_h + dh_part

        grad_h, dw_acc = bwd_update(weight, 0)
        final_state = lax.fori_loop(1, groups, bwd_body, (weight, dw_acc, grad_h))
        grad_w = lax.ppermute(final_state[1], "fsdp", ring_pairs)
        return loss_val, final_state[2], grad_w

    return jax.shard_map(local_head, mesh=mesh, in_specs=(tok_spec, P(("dp", "fsdp")), P("fsdp", None)), out_specs=(P("dp"), tok_spec, tok_spec), check_vma=False)
```

profile of v0, /device:TPU:0, one launch (start us, length us, event | category | flops | bytes accessed | tf_op | source)
XLA Modules:
  0.0 1663.4 jit_solution(4826937078884935559)
XLA Ops:
  0.6 0.0 copy-start.1
  0.6 7.2 copy.35
  7.8 7.2 copy.7
  15.0 0.0 copy-done.1
  15.0 0.0 copy-start
  15.0 18.4 %fusion.7 = (f32[1024]{0:T(1024)S(1)}, f32[1024,8032]{0,1:T(8,128)}) fusion(bf16[1024,512]{1,0:T(8,128)(2,1)S(1)} %copy-done.1, bf16[8032,512]{1,0:T(8,128)(2,1)} %copy.35), kind=kOutput, calls=%fused_computation.23 | convolution fusion | flops 8430386176 | bytes 42176512 | tf_op jit(solution)/shard_map/dot_general | solution.py:21
  33.4 0.0 copy-done
  33.4 14.8 select_reduce_fusion.1
  48.3 396.0 %while.42 = (s32[]{:T(128)}, bf16[8032,512]{1,0:T(8,128)(2,1)}, f32[1024]{0:T(1024)S(1)}, f32[1024]{0:T(1024)S(1)}, f32[1024]{0:T(1024)S(1)}, /*index=5*/bf16[10...) while((s32[]{:T(128)}, bf16[8032,512]{1,0:T(8,128)(2,1)}, ...), condition=%wide.region_7.8_spmd.clone, body=%wide.region_3.7_spmd.clone.sunk | while | flops 8471514112 | bytes 124502320 | solution.py:40
  48.3 0.9 collective-permute-start
  49.2 91.3 %collective-permute-done = bf16[8032,512]{1,0:T(8,128)(2,1)} collective-permute-done((bf16[8032,512]{1,0:T(8,128)(2,1)}, bf16[8032,512]{1,0:T(8,128)(2,1)}, u32[]{:S(2)}, u32[]{:S(2)}) %collective-permute-start) | collective-permute-done | bytes 8224800 | tf_op jit(solution)/shard_map/while/body/eval_jaxpr/ppermute | solution.py:35
  140.5 18.4 %fusion.31 = (f32[1024]{0:T(1024)S(1)}, f32[1024,8032]{0,1:T(8,128)}) fusion(bf16[1024,512]{1,0:T(8,128)(2,1)S(1)} %get-tuple-element.668, bf16[8032,512]{1,0:T(8,128)(2,1)} %collective-permute-done), kind=kOutput, calls=%fused_computation.22.clone.1 | convolution fusion | flops 8430386176 | bytes 42176512 | tf_op jit(solution)/shard_map/while/body/eval_jaxpr/dot_general | solution.py:21
  158.9 14.8 select_reduce_fusion.3
  173.8 7.2 copy.17
  181.0 0.0 collective-permute-start
  181.0 91.1 %collective-permute-done = bf16[8032,512]{1,0:T(8,128)(2,1)} collective-permute-done((bf16[8032,512]{1,0:T(8,128)(2,1)}, bf16[8032,512]{1,0:T(8,128)(2,1)}, u32[]{:S(2)}, u32[]{:S(2)}) %collective-permute-start) | collective-permute-done | bytes 8224800 | tf_op jit(solution)/shard_map/while/body/eval_jaxpr/ppermute | solution.py:35
  272.1 18.4 %fusion.31 = (f32[1024]{0:T(1024)S(1)}, f32[1024,8032]{0,1:T(8,128)}) fusion(bf16[1024,512]{1,0:T(8,128)(2,1)S(1)} %get-tuple-element.668, bf16[8032,512]{1,0:T(8,128)(2,1)} %collective-permute-done), kind=kOutput, calls=%fused_computation.22.clone.1 | convolution fusion | flops 8430386176 | bytes 42176512 | tf_op jit(solution)/shard_map/while/body/eval_jaxpr/dot_general | solution.py:21
  290.5 14.8 select_reduce_fusion.3
  305.4 7.2 copy.17
  312.6 0.0 collective-permute-start
  312.6 91.1 %collective-permute-done = bf16[8032,512]{1,0:T(8,128)(2,1)} collective-permute-done((bf16[8032,512]{1,0:T(8,128)(2,1)}, bf16[8032,512]{1,0:T(8,128)(2,1)}, u32[]{:S(2)}, u32[]{:S(2)}) %collective-permute-start) | collective-permute-done | bytes 8224800 | tf_op jit(solution)/shard_map/while/body/eval_jaxpr/ppermute | solution.py:35
  403.7 18.4 %fusion.31 = (f32[1024]{0:T(1024)S(1)}, f32[1024,8032]{0,1:T(8,128)}) fusion(bf16[1024,512]{1,0:T(8,128)(2,1)S(1)} %get-tuple-element.668, bf16[8032,512]{1,0:T(8,128)(2,1)} %collective-permute-done), kind=kOutput, calls=%fused_computation.22.clone.1 | convolution fusion | flops 8430386176 | bytes 42176512 | tf_op jit(solution)/shard_map/while/body/eval_jaxpr/dot_general | solution.py:21
  422.2 14.8 select_reduce_fusion.3
  437.1 7.2 copy.17
  444.3 0.6 subtract_reduce_fusion
  444.9 17.4 %fusion.4 = f32[1024,512]{1,0:T(8,128)S(1)} fusion(bf16[8032,512]{1,0:T(8,128)(2,1)} %copy.35, f32[1024,8032]{0,1:T(8,128)} %get-tuple-element.530, f32[1024]{0:T(1024)S(1)} %get-tuple-element.681, s32[1024]{0:T(1024)S(1)} %broadcast_subtract_fusion.2), kind=kOutput, calls=%fused_computation.20 | convolution fusion | flops 8471511040 | bytes 43229184 | tf_op jit(solution)/shard_map/dot_general | solution.py:47
  462.3 19.6 %fusion.5 = f32[8032,512]{1,0:T(8,128)} fusion(bf16[1024,512]{1,0:T(8,128)(2,1)S(1)} %get-tuple-element.726, f32[1024,8032]{0,1:T(8,128)} %get-tuple-element.530, f32[1024]{0:T(1024)S(1)} %get-tuple-element.681, s32[1024]{0:T(1024)S(1)} %broadcast_subtract_fusion.2), kind=kOutput, calls=%fused_computation.21 | convolution fusion | flops 8471511040 | bytes 50405376 | tf_op jit(solution)/shard_map/dot_general | solution.py:48
  481.9 988.8 %while.43 = (s32[]{:T(128)}, bf16[8032,512]{1,0:T(8,128)(2,1)}, f32[8032,512]{1,0:T(8,128)}, f32[1024,512]{1,0:T(8,128)S(1)}, bf16[1024,512]{1,0:T(8,128)(2,1)S(...) while((s32[]{:T(128)}, bf16[8032,512]{1,0:T(8,128)(2,1)}, ...), condition=%wide.region_11.12_spmd.clone, body=%wide.region_10.11_spmd.clone.sunk | while | flops 25320472576 | bytes 220152176 | solution.py:59
  482.1 0.0 collective-permute-start.2
  482.1 2.4 collective-permute-start.1
  484.5 265.0 %collective-permute-done.1 = bf16[8032,512]{1,0:T(8,128)(2,1)} collective-permute-done((bf16[8032,512]{1,0:T(8,128)(2,1)}, bf16[8032,512]{1,0:T(8,128)(2,1)}, u32[]{:S(2)}, u32[]{:S(2)}) %collective-permute-start.1) | collective-permute-done | bytes 8224800 | tf_op jit(solution)/shard_map/while/body/eval_jaxpr/ppermute | solution.py:53
  749.5 7.1 copy.30
  756.5 20.6 %multiply_convert_fusion.5 = bf16[1024,8032]{0,1:T(8,128)(2,1)} fusion(bf16[1024,512]{1,0:T(8,128)(2,1)S(1)} %get-tuple-element.706, bf16[8032,512]{1,0:T(8,128)(2,1)} %collective-permute-done.1, s32[1024]{0:T(1024)S(1)} %broadcast_subtract_fusion.6, f32[1024]{0:T(1024)S(1)} %get-tuple-element.707), kind=kOutput, calls=%fused_computation.8.clone.1 | convolution fusion | flops 8471511040 | bytes 25731072 | tf_op jit(solution)/shard_map/while/body/eval_jaxpr/dot_general | solution.py:21
  777.1 14.0 convolution_add_fusion.5
  791.2 0.0 collective-permute-done.2
  791.2 20.4 %convolution_add_fusion.4 = f32[8032,512]{1,0:T(8,128)} fusion(f32[8032,512]{1,0:T(8,128)} %collective-permute-done.2, bf16[1024,8032]{0,1:T(8,128)(2,1)} %multiply_convert_fusion.5, bf16[1024,512]{1,0:T(8,128)(2,1)S(1)} %get-tuple-element.706), kind=kOutput, calls=%fused_computation.9.clone.1 | convolution fusion | flops 8426274816 | bytes 50397184 | tf_op jit(solution)/shard_map/while/body/eval_jaxpr/dot_general | solution.py:48
  811.6 0.0 collective-permute-start.2
  811.6 2.4 collective-permute-start.1
  814.0 265.0 %collective-permute-done.1 = bf16[8032,512]{1,0:T(8,128)(2,1)} collective-permute-done((bf16[8032,512]{1,0:T(8,128)(2,1)}, bf16[8032,512]{1,0:T(8,128)(2,1)}, u32[]{:S(2)}, u32[]{:S(2)}) %collective-permute-start.1) | collective-permute-done | bytes 8224800 | tf_op jit(solution)/shard_map/while/body/eval_jaxpr/ppermute | solution.py:53
  1079.0 7.1 copy.30
  1086.1 20.6 %multiply_convert_fusion.5 = bf16[1024,8032]{0,1:T(8,128)(2,1)} fusion(bf16[1024,512]{1,0:T(8,128)(2,1)S(1)} %get-tuple-element.706, bf16[8032,512]{1,0:T(8,128)(2,1)} %collective-permute-done.1, s32[1024]{0:T(1024)S(1)} %broadcast_subtract_fusion.6, f32[1024]{0:T(1024)S(1)} %get-tuple-element.707), kind=kOutput, calls=%fused_computation.8.clone.1 | convolution fusion | flops 8471511040 | bytes 25731072 | tf_op jit(solution)/shard_map/while/body/eval_jaxpr/dot_general | solution.py:21
  1106.6 14.0 convolution_add_fusion.5
  1120.7 0.0 collective-permute-done.2
  1120.7 20.4 %convolution_add_fusion.4 = f32[8032,512]{1,0:T(8,128)} fusion(f32[8032,512]{1,0:T(8,128)} %collective-permute-done.2, bf16[1024,8032]{0,1:T(8,128)(2,1)} %multiply_convert_fusion.5, bf16[1024,512]{1,0:T(8,128)(2,1)S(1)} %get-tuple-element.706), kind=kOutput, calls=%fused_computation.9.clone.1 | convolution fusion | flops 8426274816 | bytes 50397184 | tf_op jit(solution)/shard_map/while/body/eval_jaxpr/dot_general | solution.py:48
  1141.1 0.0 collective-permute-start.2
  1141.1 2.4 collective-permute-start.1
  1143.5 265.0 %collective-permute-done.1 = bf16[8032,512]{1,0:T(8,128)(2,1)} collective-permute-done((bf16[8032,512]{1,0:T(8,128)(2,1)}, bf16[8032,512]{1,0:T(8,128)(2,1)}, u32[]{:S(2)}, u32[]{:S(2)}) %collective-permute-start.1) | collective-permute-done | bytes 8224800 | tf_op jit(solution)/shard_map/while/body/eval_jaxpr/ppermute | solution.py:53
  1408.5 7.1 copy.30
  1415.6 20.6 %multiply_convert_fusion.5 = bf16[1024,8032]{0,1:T(8,128)(2,1)} fusion(bf16[1024,512]{1,0:T(8,128)(2,1)S(1)} %get-tuple-element.706, bf16[8032,512]{1,0:T(8,128)(2,1)} %collective-permute-done.1, s32[1024]{0:T(1024)S(1)} %broadcast_subtract_fusion.6, f32[1024]{0:T(1024)S(1)} %get-tuple-element.707), kind=kOutput, calls=%fused_computation.8.clone.1 | convolution fusion | flops 8471511040 | bytes 25731072 | tf_op jit(solution)/shard_map/while/body/eval_jaxpr/dot_general | solution.py:21
  1436.2 14.0 convolution_add_fusion.5
  1450.2 0.0 collective-permute-done.2
  1450.2 20.4 %convolution_add_fusion.4 = f32[8032,512]{1,0:T(8,128)} fusion(f32[8032,512]{1,0:T(8,128)} %collective-permute-done.2, bf16[1024,8032]{0,1:T(8,128)(2,1)} %multiply_convert_fusion.5, bf16[1024,512]{1,0:T(8,128)(2,1)S(1)} %get-tuple-element.706), kind=kOutput, calls=%fused_computation.9.clone.1 | convolution fusion | flops 8426274816 | bytes 50397184 | tf_op jit(solution)/shard_map/while/body/eval_jaxpr/dot_general | solution.py:48
  1470.7 0.0 copy-start.2
  1470.7 0.0 collective-permute-start.3
  1471.3 180.0 %psum.7 = f32[1]{0:T(128)} all-reduce(f32[1]{0:T(128)} %bitcast), channel_id=1, replica_groups=mesh['dp'=2,'fsdp'=4] {'fsdp'}, use_global_device_ids=true, to_apply=%region_9.10 | all-reduce | flops 1 | bytes 8 | tf_op jit(solution)/shard_map/psum | solution.py:42
  1651.3 0.0 collective-permute-done.3
  1651.3 11.6 copy.36
  1663.0 0.0 copy-done.2
  (20 shorter events, 0.1 us)
Async XLA Ops:
  0.6 14.4 copy-start.1
  15.0 18.4 %copy-start = (s32[1024]{0:T(1024)S(1)}, s32[1024]{0:T(1024)}, u32[]{:S(2)}) copy-start(s32[1024]{0:T(1024)} %param.8) | copy-start | bytes 12292
  48.3 92.2 %collective-permute-start = (bf16[8032,512]{1,0:T(8,128)(2,1)}, bf16[8032,512]{1,0:T(8,128)(2,1)}, u32[]{:S(2)}, u32[]{:S(2)}) collective-permute-start(bf16[8032,512]{1,0:T(8,128)(2,1)} %get-tuple-element.651), channel_id=1, source_target_pairs={{0,1},{1,2},{2,3},{3,0},{4,5},{5,6},{6,7},{7,4}} | collective-permute-start | bytes 24674312 | tf_op jit(solution)/shard_map/while/body/eval_jaxpr/ppermute | solution.py:35
  181.0 91.1 %collective-permute-start = (bf16[8032,512]{1,0:T(8,128)(2,1)}, bf16[8032,512]{1,0:T(8,128)(2,1)}, u32[]{:S(2)}, u32[]{:S(2)}) collective-permute-start(bf16[8032,512]{1,0:T(8,128)(2,1)} %get-tuple-element.651), channel_id=1, source_target_pairs={{0,1},{1,2},{2,3},{3,0},{4,5},{5,6},{6,7},{7,4}} | collective-permute-start | bytes 24674312 | tf_op jit(solution)/shard_map/while/body/eval_jaxpr/ppermute | solution.py:35
  312.6 91.1 %collective-permute-start = (bf16[8032,512]{1,0:T(8,128)(2,1)}, bf16[8032,512]{1,0:T(8,128)(2,1)}, u32[]{:S(2)}, u32[]{:S(2)}) collective-permute-start(bf16[8032,512]{1,0:T(8,128)(2,1)} %get-tuple-element.651), channel_id=1, source_target_pairs={{0,1},{1,2},{2,3},{3,0},{4,5},{5,6},{6,7},{7,4}} | collective-permute-start | bytes 24674312 | tf_op jit(solution)/shard_map/while/body/eval_jaxpr/ppermute | solution.py:35
  482.1 309.1 %collective-permute-start.2 = (f32[8032,512]{1,0:T(8,128)}, f32[8032,512]{1,0:T(8,128)}, u32[]{:S(2)}, u32[]{:S(2)}) collective-permute-start(f32[8032,512]{1,0:T(8,128)} %get-tuple-element.691), channel_id=1, source_target_pairs={{0,1},{1,2},{2,3},{3,0},{4,5},{5,6},{6,7},{7,4}} | collective-permute-start | bytes 49348616 | tf_op jit(solution)/shard_map/while/body/eval_jaxpr/ppermute | solution.py:54
  482.1 267.4 %collective-permute-start.1 = (bf16[8032,512]{1,0:T(8,128)(2,1)}, bf16[8032,512]{1,0:T(8,128)(2,1)}, u32[]{:S(2)}, u32[]{:S(2)}) collective-permute-start(bf16[8032,512]{1,0:T(8,128)(2,1)} %get-tuple-element.690), channel_id=1, source_target_pairs={{0,1},{1,2},{2,3},{3,0},{4,5},{5,6},{6,7},{7,4}} | collective-permute-start | bytes 24674312 | tf_op jit(solution)/shard_map/while/body/eval_jaxpr/ppermute | solution.py:53
  811.6 309.1 %collective-permute-start.2 = (f32[8032,512]{1,0:T(8,128)}, f32[8032,512]{1,0:T(8,128)}, u32[]{:S(2)}, u32[]{:S(2)}) collective-permute-start(f32[8032,512]{1,0:T(8,128)} %get-tuple-element.691), channel_id=1, source_target_pairs={{0,1},{1,2},{2,3},{3,0},{4,5},{5,6},{6,7},{7,4}} | collective-permute-start | bytes 49348616 | tf_op jit(solution)/shard_map/while/body/eval_jaxpr/ppermute | solution.py:54
  811.6 267.4 %collective-permute-start.1 = (bf16[8032,512]{1,0:T(8,128)(2,1)}, bf16[8032,512]{1,0:T(8,128)(2,1)}, u32[]{:S(2)}, u32[]{:S(2)}) collective-permute-start(bf16[8032,512]{1,0:T(8,128)(2,1)} %get-tuple-element.690), channel_id=1, source_target_pairs={{0,1},{1,2},{2,3},{3,0},{4,5},{5,6},{6,7},{7,4}} | collective-permute-start | bytes 24674312 | tf_op jit(solution)/shard_map/while/body/eval_jaxpr/ppermute | solution.py:53
  1141.1 309.1 %collective-permute-start.2 = (f32[8032,512]{1,0:T(8,128)}, f32[8032,512]{1,0:T(8,128)}, u32[]{:S(2)}, u32[]{:S(2)}) collective-permute-start(f32[8032,512]{1,0:T(8,128)} %get-tuple-element.691), channel_id=1, source_target_pairs={{0,1},{1,2},{2,3},{3,0},{4,5},{5,6},{6,7},{7,4}} | collective-permute-start | bytes 49348616 | tf_op jit(solution)/shard_map/while/body/eval_jaxpr/ppermute | solution.py:54
  1141.1 267.4 %collective-permute-start.1 = (bf16[8032,512]{1,0:T(8,128)(2,1)}, bf16[8032,512]{1,0:T(8,128)(2,1)}, u32[]{:S(2)}, u32[]{:S(2)}) collective-permute-start(bf16[8032,512]{1,0:T(8,128)(2,1)} %get-tuple-element.690), channel_id=1, source_target_pairs={{0,1},{1,2},{2,3},{3,0},{4,5},{5,6},{6,7},{7,4}} | collective-permute-start | bytes 24674312 | tf_op jit(solution)/shard_map/while/body/eval_jaxpr/ppermute | solution.py:53
  1470.7 192.3 %copy-start.2 = (f32[1024,512]{1,0:T(8,128)}, f32[1024,512]{1,0:T(8,128)S(1)}, u32[]{:S(2)}) copy-start(f32[1024,512]{1,0:T(8,128)S(1)} %get-tuple-element.719) | copy-start | bytes 6291460
  1470.7 180.7 %collective-permute-start.3 = (f32[8032,512]{1,0:T(8,128)}, f32[8032,512]{1,0:T(8,128)}, u32[]{:S(2)}, u32[]{:S(2)}) collective-permute-start(f32[8032,512]{1,0:T(8,128)} %get-tuple-element.452), channel_id=1, source_target_pairs={{0,1},{1,2},{2,3},{3,0},{4,5},{5,6},{6,7},{7,4}} | collective-permute-start | bytes 49348616 | tf_op jit(solution)/shard_map/ppermute | solution.py:60
where the time goes:
time: 1680 us; the launch traced here: 1660 us
  waiting for transfers between devices  1070 us (64%)
  matrix products  276 us (16%)
  blocking collectives  180 us (11%)
  local copies, waits for them, and re-layouts  68.9 us (4%)
  other arithmetic  60.1 us (4%)
    ppermute x3, waiting for transfers between devices, bwd_body(): w_cur = lax.ppermute(w_cur, 'fsdp', ring_pairs)  795 us
    ppermute x3, waiting for transfers between devices, fwd_body(): w_cur = lax.ppermute(w_cur, 'fsdp', ring_pairs)  274 us
    psum x1, blocking collectives, local_head(): lax.psum(jnp.sum(log_norm - tgt_logit) / tokens, 'fsdp').reshape(1)  180 us
    dot_general x7, matrix products, block_logits(): lax.dot_general(hidden, w_blk, (((1,), (1,)), ((), ())), preferred_elemen...  135 us
    dot_general x4, matrix products, bwd_update(): lax.dot_general(dlogits, hidden, (((0,), (0,)), ((), ())), preferred_elem...  80.8 us
    dot_general x4, matrix products, bwd_update(): dh_part = jnp.dot(dlogits, w_blk, preferred_element_type=jnp.float32)  59.5 us
    reduce_sum x4, other arithmetic, fwd_update(): tgt_logit = tgt_logit + jnp.sum(jnp.where(is_target, logits, 0.0), axis=1)  59.4 us
    while x9, local copies, waits for them, and re-layouts  42.9 us
  transfers between devices with their start and end apart: 10, of which 6 were waited for; matrix products, arithmetic and copies ran while one was open for 8% of the time, Pallas kernels for 0%

commit v1 on v0

v1 whole, which is shorter than its diff:
```python
import jax
import jax.numpy as jnp
from jax import lax
from jax.experimental import pallas as pl
from jax.experimental.pallas import tpu as pltpu
from jax.sharding import PartitionSpec as P

SUB = 256
UNROLL_F = 14
UNROLL_B = 28
f32 = jnp.float32
bf16 = jnp.bfloat16


def _nn(a, b):
    return lax.dot_general(a, b, (((1,), (0,)), ((), ())), preferred_element_type=f32)


def _tn(a, b):
    return lax.dot_general(a, b, (((0,), (0,)), ((), ())), preferred_element_type=f32)


def _pipeline(step, steps, unroll):
    loops = (steps - 1) // unroll

    @pl.loop(0, loops)
    def _(i):
        for u in range(unroll):
            step(1 + i * unroll + u, (1 + u) % 2)

    for k in range(1 + loops * unroll, steps):
        step(k, k % 2)


def _fwd_kernel(w_ref, h_ref, m_ref, s_ref, ht, z0, z1, m8, s8):
    vloc, depth = w_ref.shape
    tok = h_ref.shape[0]
    full, rem = vloc // SUB, vloc % SUB
    zbuf = (z0, z1)

    def zdot(k, slot, rows=SUB):
        zbuf[slot][pl.ds(0, rows), :] = _nn(w_ref[pl.ds(k * SUB, rows), :], ht[...])

    def epi(slot, rows=SUB):
        z = zbuf[slot][pl.ds(0, rows), :].reshape(rows // 8, 8, tok)
        old = m8[...]
        new = jnp.maximum(old, jnp.max(z, axis=0))
        s8[...] = s8[...] * jnp.exp(old - new) + jnp.sum(jnp.exp(z - new[None]), axis=0)
        m8[...] = new

    ht[...] = h_ref[...].T
    m8[...] = jnp.full(m8.shape, -jnp.inf, f32)
    s8[...] = jnp.zeros(s8.shape, f32)

    def step(k, par, zrows=SUB, erows=SUB):
        if zrows:
            zdot(k + 1, 1 - par, zrows)
        if erows:
            epi(par, erows)

    zdot(0, 0)
    step(0, 0)
    _pipeline(step, full - 1, UNROLL_F)
    step(full - 1, (full - 1) % 2, zrows=rem)
    if rem:
        step(full, full % 2, zrows=0, erows=rem)
    top = jnp.max(m8[...], axis=0, keepdims=True)
    m_ref[...] = top
    s_ref[...] = jnp.sum(s8[...] * jnp.exp(m8[...] - top), axis=0, keepdims=True)


def _bwd_kernel(w_ref, h_ref, lse_ref, tgt_ref, dw_ref, dh_ref, zt_ref, ht, dht, z0, z1, g0, g1):
    chunk = pl.program_id(0)
    vloc, depth = w_ref.shape
    tok = h_ref.shape[0]
    full, rem = vloc // SUB, vloc % SUB
    zbuf, gbuf = (z0, z1), (g0, g1)
    scale = 1.0 / (tok * pl.num_programs(0))

    def zdot(k, slot, rows=SUB):
        zbuf[slot][pl.ds(0, rows), :] = _nn(w_ref[pl.ds(k * SUB, rows), :], ht[...])

    def epi(k, slot, rows=SUB):
        z = zbuf[slot][pl.ds(0, rows), :]
        hit = lax.broadcasted_iota(jnp.int32, (rows, tok), 0) == tgt_ref[...] - k * SUB
        p = jnp.exp(z - lse_ref[...])
        zt_ref[...] += jnp.sum(jnp.where(hit, z, 0.0), axis=0, keepdims=True)
        gbuf[slot][pl.ds(0, rows), :] = ((p - jnp.where(hit, 1.0, 0.0)) * (1.0 / 4096.0)).astype(bf16)

    def ddot(k, slot, rows=SUB):
        g = gbuf[slot][pl.ds(0, rows), :]
        rng = pl.ds(k * SUB, rows)
        dw_ref[rng, :] = dw_ref[rng, :] + _nn(g, h_ref[...])
        dht[...] += _tn(w_ref[rng, :], g)

    @pl.when(chunk == 0)
    def _():
        @pl.loop(0, vloc // 32)
        def _(i):
            dw_ref[pl.ds(i * 32, 32), :] = jnp.zeros((32, depth), f32)

    ht[...] = h_ref[...].T
    dht[...] = jnp.zeros(dht.shape, f32)
    zt_ref[...] = jnp.zeros(zt_ref.shape, f32)

    def step(k, par, zrows=SUB, erows=SUB, drows=SUB):
        if drows:
            ddot(k - 1, 1 - par, drows)
        if zrows:
            zdot(k + 1, 1 - par, zrows)
        if erows:
            epi(k, par, erows)

    zdot(0, 0)
    step(0, 0, drows=0)
    _pipeline(step, full - 1, UNROLL_B)
    step(full - 1, (full - 1) % 2, zrows=rem)
    step(full, full % 2, zrows=0, erows=rem)
    if rem:
        step(full + 1, (full + 1) % 2, zrows=0, erows=0, drows=rem)
    dh_ref[...] = dht[...].T


def solution(mesh):
    groups = mesh.shape["fsdp"]
    tok_spec = P(("dp", "fsdp"), None)

    def local_head(hidden, targets, weight):
        tok, depth = hidden.shape
        vloc = weight.shape[0]
        total = tok * groups
        rank = lax.axis_index("fsdp")
        h_all = lax.all_gather(hidden, "fsdp", axis=0, tiled=True)
        t_all = lax.all_gather(targets, "fsdp", axis=0, tiled=True)
        row = lambda c: (0, c)
        whole = lambda c: (0, 0)
        params = pltpu.CompilerParams(vmem_limit_bytes=66_000_000, dimension_semantics=("arbitrary",))
        m, s = pl.pallas_call(
            _fwd_kernel,
            grid=(groups,),
            in_specs=[pl.BlockSpec((vloc, depth), whole), pl.BlockSpec((tok, depth), lambda c: (c, 0))],
            out_specs=[pl.BlockSpec((1, tok), row)] * 2,
            out_shape=[jax.ShapeDtypeStruct((1, total), f32)] * 2,
            scratch_shapes=[pltpu.VMEM((depth, tok), bf16)] + [pltpu.VMEM((SUB, tok), f32)] * 2 + [pltpu.VMEM((8, tok), f32)] * 2,
            compiler_params=params,
            name="ce_fwd",
        )(weight, h_all)
        ms = lax.all_gather(jnp.concatenate([m, s], axis=0), "fsdp")
        top = jnp.max(ms[:, 0], axis=0)
        lse = top + jnp.log(jnp.sum(ms[:, 1] * jnp.exp(ms[:, 0] - top), axis=0))
        dw, dh, zt = pl.pallas_call(
            _bwd_kernel,
            grid=(groups,),
            in_specs=[
                pl.BlockSpec((vloc, depth), whole),
                pl.BlockSpec((tok, depth), lambda c: (c, 0)),
                pl.BlockSpec((1, tok), row),
                pl.BlockSpec((1, tok), row),
            ],
            out_specs=[pl.BlockSpec((vloc, depth), whole), pl.BlockSpec((tok, depth), lambda c: (c, 0)), pl.BlockSpec((1, tok), row)],
            out_shape=[
                jax.ShapeDtypeStruct((vloc, depth), f32),
                jax.ShapeDtypeStruct((total, depth), f32),
                jax.ShapeDtypeStruct((1, total), f32),
            ],
            scratch_shapes=[pltpu.VMEM((depth, tok), bf16), pltpu.VMEM((depth, tok), f32)]
            + [pltpu.VMEM((SUB, tok), f32)] * 2
            + [pltpu.VMEM((SUB, tok), bf16)] * 2,
            compiler_params=params,
            name="ce_bwd",
        )(weight, h_all, lse[None, :], (t_all - rank * vloc)[None, :])
        grad_h = lax.psum_scatter(dh, "fsdp", scatter_dimension=0, tiled=True)
        loss = lax.psum(jnp.sum(lse) / groups - jnp.sum(zt), "fsdp") / total
        return loss.reshape(1), grad_h, dw

    return jax.shard_map(local_head, mesh=mesh, in_specs=(tok_spec, P(("dp", "fsdp")), P("fsdp", None)), out_specs=(P("dp"), tok_spec, tok_spec), check_vma=False)
```

time: 1680 us -> 298 us (0.18)
  waiting for transfers between devices: 1070 us -> 83.6 us
  matrix products: 276 us -> 0 us
  Pallas kernels: 0 us -> 170 us
  blocking collectives: 180 us -> 23.5 us
  local copies, waits for them, and re-layouts: 68.9 us -> 0.05 us
  other arithmetic: 60.1 us -> 3.47 us
    ppermute x10 -> x0, waiting for transfers between devices: 1070 us -> none  [the longest x3 795 us: bwd_body(): w_cur = lax.ppermute(w_cur, 'fsdp', ring_pairs)]
    dot_general x15 -> x0, matrix products: 276 us -> none  [the longest x7 135 us: block_logits(): lax.dot_general(hidden, w_blk, (((1,), (1,)), ((), ())), preferred_elemen...]
    psum x1, blocking collectives: 180 us -> 6.17 us  [local_head(): loss = lax.psum(jnp.sum(lse) / groups - jnp.sum(zt), 'fsdp') / total]
    pallas_call x0 -> x2, Pallas kernels: none -> 170 us  [the longest x1 125 us: local_head(): pl.pallas_call(_bwd_kernel, grid=(groups,), in_specs=[pl.BlockSpec((vloc,...]
    reduce_sum x5 -> x3, other arithmetic: 60 us -> 1.97 us  [the longest x2 1.85 us: local_head(): loss = lax.psum(jnp.sum(lse) / groups - jnp.sum(zt), 'fsdp') / total]
    reduce_scatter x0 -> x1, waiting for transfers between devices: none -> 57.6 us  [local_head(): grad_h = lax.psum_scatter(dh, 'fsdp', scatter_dimension=0, tiled=True)]
    while x9 -> x0, local copies, waits for them, and re-layouts: 42.9 us -> none
    unnamed x9 -> x2, local copies, waits for them, and re-layouts: 26 us -> 0.05 us
  transfers between devices with their start and end apart: 10 -> 2, of which waited for: 6 -> 2; matrix products, arithmetic and copies ran while one was open for 8% -> 0% of each run, Pallas kernels for 0% -> 0%
where the time goes in v1:
time: 298 us
  Pallas kernels  170 us (57%)
  waiting for transfers between devices  83.6 us (28%)
  blocking collectives  23.5 us (8%)
  between operations  17.1 us (6%)
  other arithmetic  3.47 us (1%)
    pallas_call x1, Pallas kernels, local_head(): pl.pallas_call(_bwd_kernel, grid=(groups,), in_specs=[pl.BlockSpec((vloc,...  125 us
    reduce_scatter x1, waiting for transfers between devices, local_head(): grad_h = lax.psum_scatter(dh, 'fsdp', scatter_dimension=0, tiled=True)  57.6 us
    pallas_call x1, Pallas kernels, local_head(): pl.pallas_call(_fwd_kernel, grid=(groups,), in_specs=[pl.BlockSpec((vloc,...  45.1 us
    all_gather x1, waiting for transfers between devices, local_head(): h_all = lax.all_gather(hidden, 'fsdp', axis=0, tiled=True)  25.3 us
    all_gather x1, blocking collectives, local_head(): t_all = lax.all_gather(targets, 'fsdp', axis=0, tiled=True)  9.98 us
    all_gather x1, blocking collectives, local_head(): ms = lax.all_gather(jnp.concatenate([m, s], axis=0), 'fsdp')  7.3 us
    psum x1, blocking collectives, local_head(): loss = lax.psum(jnp.sum(lse) / groups - jnp.sum(zt), 'fsdp') / total  6.17 us
  transfers between devices with their start and end apart: 2, of which 2 were waited for; matrix products, arithmetic and copies ran while one was open for 0% of the time, Pallas kernels for 0%

profile of v1, /device:TPU:0, one launch (start us, length us, event | category | flops | bytes accessed | tf_op | source)
XLA Modules:
  0.0 297.6 jit_solution(8701035953157303447)
XLA Ops:
  7.2 0.0 all-gather.4.cloned.1.call-start
  7.2 0.7 all-gather.4.cloned.1.call-update
  7.9 0.0 reduce-scatter.2.cloned.1.call-start
  7.9 10.0 %all_gather.15 = s32[4096]{0:T(1024)S(1)} all-gather(s32[1024]{0:T(1024)} %param.4), channel_id=1, replica_groups=mesh['dp'=2,'fsdp'=4] {'fsdp'}, dimensions={0}, use_global_device_ids=true | all-gather | bytes 20480 | tf_op jit(solution)/shard_map/all_gather | solution.py:134
  17.9 0.6 broadcast_subtract_fusion
  18.5 25.3 %all-gather.4.cloned.1.call-done.h_ref = bf16[4096,512]{1,0:T(8,128)(2,1)} async-done(((bf16[1024,512]{1,0:T(8,128)(2,1)}), bf16[4096,512]{1,0:T(8,128)(2,1)}) %all-gather.4.cloned.1.call-update) | async-done | bytes 4194320 | tf_op jit(solution)/shard_map/all_gather | solution.py:133
  43.9 45.1 %ce_fwd.1 = (f32[1,4096]{1,0:T(1,128)}, f32[1,4096]{1,0:T(1,128)}) custom-call(bf16[8032,512]{1,0:T(8,128)(2,1)} %w_ref.3, bf16[4096,512]{1,0:T(8,128)(2,1)} %all-gather.4.cloned.1.call-done.h_ref), custom_call_target="tpu_custom_call" | custom-call | tf_op jit(solution)/shard_map/ce_fwd/pallas_call | solution.py:138
  88.9 0.8 maximum_bitcast_fusion
  89.7 7.3 %all-gather.1 = f32[4,2,4096]{2,1,0:T(2,128)S(1)} all-gather(f32[1,2,4096]{2,1,0:T(2,128)S(1)} %maximum_bitcast_fusion), channel_id=2, replica_groups=mesh['dp'=2,'fsdp'=4] {'fsdp'}, dimensions={0}, use_global_device_ids=true | all-gather | bytes 163840 | tf_op jit(solution)/shard_map/all_gather | solution.py:148
  97.0 0.1 fusion.4
  97.1 0.1 fusion.1
  97.3 1.2 fusion.3
  98.5 124.7 %ce_bwd.1 = (f32[8032,512]{1,0:T(8,128)}, f32[4096,512]{1,0:T(8,128)}, f32[1,4096]{1,0:T(1,128)}) custom-call(bf16[8032,512]{1,0:T(8,128)(2,1)} %w_ref.3, bf16[4096,512]{1,0:T(8,128)(2,1)} %all-gather.4.cloned.1.call-done.h_ref, f32[1,4096]{1,0:T(1,128)} %bitcast.17, s32[1,4096]{1,0:T(1,128)} %bitcast.18), custom_call_target="tpu_custom_call" | custom-call | tf_op jit(solution)/shard_map/ce_bwd/pallas_call | solution.py:151
  223.2 0.0 copy-start
  223.2 0.0 reduce-scatter.2.cloned.1.call-update
  223.9 0.0 copy-done
  223.9 0.6 reduce_sum.29
  225.2 6.2 %psum.7 = f32[]{:T(128)} all-reduce(f32[]{:T(128)S(6)} %sub.21), channel_id=1, replica_groups=mesh['dp'=2,'fsdp'=4] {'fsdp'}, use_global_device_ids=true, to_apply=%region_4.0 | all-reduce | flops 1 | bytes 8 | tf_op jit(solution)/shard_map/psum | solution.py:173
  232.0 57.6 %reduce-scatter.2.cloned.1.call-done = f32[1024,512]{1,0:T(8,128)} async-done(((f32[4096,512]{1,0:T(8,128)}), f32[1024,512]{1,0:T(8,128)}) %reduce-scatter.2.cloned.1.call-update) | async-done | bytes 2097168 | tf_op jit(solution)/shard_map/reduce_scatter | solution.py:172
Async XLA Ops:
  7.2 36.7 %all-gather.4.cloned.1.call-start = ((), (), s32[]{:S(2)}) async-start(), calls=%async_computation.1 | async-start | bytes 5242880 | tf_op jit(solution)/shard_map/all_gather | solution.py:133
  7.9 281.7 %reduce-scatter.2.cloned.1.call-start = ((), (), s32[]{:S(2)}) async-start(), calls=%async_computation.2 | async-start | bytes 10485760 | tf_op jit(solution)/shard_map/reduce_scatter | solution.py:172
  223.2 0.7 copy-start
Sparse Core Ops, SparseCore 0:
  9.5 34.3 all-gather.3
  223.3 66.2 reduce-scatter.1
